TPU v7x, 128 devices: a whole 4x4x4 slice. The times are simulated.
128 devices in a mesh: tp: 4 (over y_hi, core), grp: 32 (over z, x, y_lo).
Axes of the slice: x: 4, y: 4 (y_hi: 2, y_lo: 2; y = y_hi * 2 + y_lo), z: 4, core: 2. Of those that a mesh axis runs over, the one named last changes fastest.
Arguments:
- teacher_state: bfloat16 [8192, 5280], P('grp'), may hold values from -6 to 6
- injection: bfloat16 [8192, 5280], P('grp'), may hold values from -6 to 6
- teacher_up: bfloat16 [5280, 8960], P(None, 'tp'), may hold values from -0.078125 to 0.078125
- teacher_down: bfloat16 [8960, 5280], P('tp', 'grp'), may hold values from -0.0625 to 0.0625
- student_up: bfloat16 [5280, 256], P('grp', 'tp'), may hold values from -0.078125 to 0.078125
- student_down: bfloat16 [256, 5280], P('tp', 'grp'), may hold values from -0.375 to 0.375
- teacher_step: int32 [8], replicated, may hold values from 0 to 1
- student_depth: int32 [8], replicated, may hold values from 1 to 2
Outputs:
- grad_up: float32 [5280, 256], P('grp', 'tp')
- grad_down: float32 [256, 5280], P('tp', 'grp')
All inputs are finite; a program needn't handle non-finite values.
Results may differ from a plain program's by a relative error of at most 0.02.
Values may be sent and summed in bfloat16 or wider, within the bound.
A program may use at most 192 MiB of HBM per device.

v0:
```python
import jax
import jax.numpy as jnp
from jax import lax
from jax.sharding import PartitionSpec as P

LENGTH = 1024
S_ITERS = 2
epsilon = 1e-06
loss_scale = 64.0


def in_order(tiles, dim):
    shape = list(tiles.shape[1:])
    shape[dim] *= tiles.shape[0]
    return jnp.moveaxis(tiles, 0, dim).reshape(shape)


def on_gathered_pieces(value, axis, dim, apply, out_dim):
    size, extent = (lax.axis_size(axis), value.shape[dim])
    count = 2 if extent % 2 == 0 else 1
    outs, length = ([], extent // count)
    for k in range(count):
        piece = lax.slice_in_dim(value, k * length, (k + 1) * length, axis=dim)
        starts = jnp.arange(size) * extent + k * length
        outs.append(jax.vmap(apply)(lax.all_gather(piece, axis), starts))
    return in_order(jnp.concatenate(outs, axis=out_dim + 1), out_dim)


def in_blocks(value, dim, size):
    shape = value.shape
    tiles = value.reshape(*shape[:dim], size, shape[dim] // size, *shape[dim + 1 :])
    return jnp.moveaxis(tiles, dim, 0)


def sent_and_summed(value, axis, dim):
    tiles = in_blocks(value, dim, lax.axis_size(axis))
    arrived = lax.all_to_all(tiles, axis, split_axis=0, concat_axis=0, tiled=True)
    return arrived.astype(jnp.float32).sum(axis=0)


def normalize(summed):
    return lax.rsqrt(jnp.mean(summed * summed, axis=-1, keepdims=True) + epsilon)


def silu_slope(logits):
    sigmoid = jax.nn.sigmoid(logits)
    return sigmoid * (1.0 + logits * (1.0 - sigmoid))


def student_grads(
    start, injection, latents, pick_teacher, pick_depth, student_up, student_down, row_count
):
    previous = start
    records = []
    outputs = []
    for iteration in range(S_ITERS):
        summed = previous.astype(jnp.float32) + injection.astype(jnp.float32)
        factor = normalize(summed)
        normed = (summed * factor).astype(jnp.bfloat16)
        logits = jnp.dot(normed, student_up, preferred_element_type=jnp.float32)
        hidden = jax.nn.silu(logits).astype(jnp.bfloat16)
        previous = (
            previous.astype(jnp.float32)
            + jnp.dot(hidden, student_down, preferred_element_type=jnp.float32)
        ).astype(jnp.bfloat16)
        records.append((summed, factor, normed, logits, hidden))
        outputs.append(previous)
    target = start.astype(jnp.float32)
    iteration = 0
    target = jnp.where(
        pick_teacher[:, None] == iteration + 1, latents[iteration].astype(jnp.float32), target
    )
    result = jnp.zeros(start.shape, jnp.float32)
    for iteration in range(S_ITERS):
        result = jnp.where(
            pick_depth[:, None] == iteration + 1, outputs[iteration].astype(jnp.float32), result
        )
    slope = loss_scale * 2.0 / row_count * (result - target)
    grad_up = jnp.zeros(student_up.shape, jnp.float32)
    grad_down = jnp.zeros(student_down.shape, jnp.float32)
    carried = jnp.zeros(start.shape, jnp.float32)
    for iteration in reversed(range(S_ITERS)):
        summed, factor, normed, logits, hidden = records[iteration]
        cotangent = carried + jnp.where(pick_depth[:, None] == iteration + 1, slope, 0.0)
        rounded = cotangent.astype(jnp.bfloat16)
        grad_down = grad_down + jnp.dot(hidden.T, rounded, preferred_element_type=jnp.float32)
        upstream = jnp.dot(rounded, student_down.T, preferred_element_type=jnp.float32)
        local_grad = (upstream * silu_slope(logits)).astype(jnp.bfloat16)
        grad_up = grad_up + jnp.dot(normed.T, local_grad, preferred_element_type=jnp.float32)
        if iteration > 0:
            back_flow = jnp.dot(local_grad, student_up.T, preferred_element_type=jnp.float32)
            carried = (
                cotangent
                + factor * back_flow
                - summed * factor**3 * jnp.mean(summed * back_flow, axis=-1, keepdims=True)
            )
    return (grad_up, grad_down)


def body(
    teacher_state,
    injection,
    teacher_up,
    teacher_down,
    student_up,
    student_down,
    teacher_step,
    student_depth,
):
    slices = lax.axis_size("tp")
    group_rows = teacher_state.shape[0]
    own_count = group_rows // slices
    row_start = lax.axis_index("tp") * own_count

    def own_rows(whole):
        return lax.dynamic_slice_in_dim(whole, row_start, own_count, 0)

    latents = []
    summed = teacher_state.astype(jnp.float32) + injection.astype(jnp.float32)
    normed = (summed * normalize(summed)).astype(jnp.bfloat16)
    hidden = jax.nn.silu(jnp.dot(normed, teacher_up, preferred_element_type=jnp.float32)).astype(
        jnp.bfloat16
    )

    def columns(piece, start):
        return jnp.dot(hidden, piece, preferred_element_type=jnp.float32)

    row_share = lax.psum_scatter(
        on_gathered_pieces(teacher_down, "grp", 1, columns, 1).astype(jnp.bfloat16),
        "tp",
        scatter_dimension=0,
        tiled=True,
    ).astype(jnp.float32)
    row_state = (own_rows(teacher_state).astype(jnp.float32) + row_share).astype(jnp.bfloat16)
    latents.append(row_state)
    gathered_up, gathered_down = (
        lax.all_gather(student_up, "grp", axis=0, tiled=True),
        lax.all_gather(student_down, "grp", axis=1, tiled=True),
    )
    gathered_up, gathered_down = (
        lax.all_gather(gathered_up, "tp", axis=1, tiled=True),
        lax.all_gather(gathered_down, "tp", axis=0, tiled=True),
    )
    first_row = lax.axis_index("grp") * group_rows + row_start
    sequence = (first_row + jnp.arange(own_count, dtype=jnp.int32)) // LENGTH
    matches = sequence[:, None] == jnp.arange(teacher_step.shape[0], dtype=jnp.int32)[None, :]
    pick_teacher = jnp.sum(jnp.where(matches, teacher_step[None, :], 0), axis=1)
    pick_depth = jnp.sum(jnp.where(matches, student_depth[None, :], 0), axis=1)
    grad_up, grad_down = student_grads(
        own_rows(teacher_state),
        own_rows(injection),
        latents,
        pick_teacher,
        pick_depth,
        gathered_up,
        gathered_down,
        group_rows * lax.axis_size("grp"),
    )
    grad_up, grad_down = (
        lax.psum_scatter(
            grad_up.astype(jnp.bfloat16), "tp", scatter_dimension=1, tiled=True
        ).astype(jnp.float32),
        lax.psum_scatter(
            grad_down.astype(jnp.bfloat16), "tp", scatter_dimension=0, tiled=True
        ).astype(jnp.float32),
    )
    grad_up, grad_down = (
        sent_and_summed(grad_up.astype(jnp.bfloat16), "grp", 0),
        sent_and_summed(grad_down.astype(jnp.bfloat16), "grp", 1),
    )
    return (grad_up, grad_down)


def solution(mesh):
    in_specs = (
        P("grp", None),
        P("grp", None),
        P(None, "tp"),
        P("tp", "grp"),
        P("grp", "tp"),
        P("tp", "grp"),
        P(),
        P(),
    )
    out_specs = (P("grp", "tp"), P("tp", "grp"))
    return jax.shard_map(body, mesh=mesh, in_specs=in_specs, out_specs=out_specs, check_vma=False)
```

profile of v0, /device:TPU:0, one launch (start us, length us, event | category | flops | bytes accessed | tf_op | source)
XLA Modules:
  0.0 828.8 jit_solution(9276407297608392390)
XLA Ops:
  7.2 0.7 all-gather.12.cloned.1.call-update
  7.9 111.7 %all-gather.1 = bf16[32,165,64]{1,2,0:T(8,128)(2,1)S(1)} all-gather(bf16[1,165,64]{1,2,0:T(8,128)(2,1)} %bitcast.37), channel_id=1, replica_groups=mesh['tp'=4,'grp'=32] {'grp'}, dimensions={0}, use_global_device_ids=true | all-gather | bytes 696960 | tf_op jit(solution)/shard_map/all_gather | solution.py:137
  119.7 0.6 copy.27
  120.3 2.3 reshape.83
  122.6 103.0 %all-gather.2 = bf16[32,165,64]{1,2,0:T(8,128)(2,1)S(1)} all-gather(bf16[1,165,64]{1,2,0:T(8,128)(2,1)S(1)} %bitcast.38), channel_id=1, replica_groups=mesh['tp'=4,'grp'=32] {'grp'}, dimensions={0}, use_global_device_ids=true | all-gather | bytes 696960 | tf_op jit(solution)/shard_map/all_gather | solution.py:138
  225.6 1.6 copy.28
  227.1 3.1 reshape.85
  230.5 2.9 multiply_reduce_fusion
  233.4 13.2 %fusion.11 = bf16[256,2240,1]{0,1,2:T(8,128)(2,1)} fusion(bf16[5280,2240]{0,1:T(8,128)(2,1)} %param.10, bf16[256,5280]{0,1:T(8,128)(2,1)S(1)} %copy-done.8, bf16[256,5280]{0,1:T(8,128)(2,1)S(1)} %copy-done.10, f32[256]{0:T(256)S(1)} %add_rsqrt_fusion), kind=kOutput, calls=%fused_computation.22 | convolution fusion | flops 6065152000 | bytes 30209024 | tf_op jit(solution)/shard_map/dot_general | solution.py:121
  246.6 337.5 %all-gather.12.cloned.1.call-done = bf16[32,2240,165]{1,2,0:T(8,128)(2,1)} async-done(((bf16[1,2240,165]{1,2,0:T(8,128)(2,1)}), bf16[32,2240,165]{1,2,0:T(8,128)(2,1)}) %all-gather.12.cloned.1.call-update) | async-done | bytes 23654416 | tf_op jit(solution)/shard_map/all_gather | solution.py:25
  584.1 12.8 %convolution_convert_fusion = bf16[256,32,165]{0,2,1:T(8,128)(2,1)} fusion(bf16[256,2240,1]{0,1,2:T(8,128)(2,1)} %fusion.11, bf16[32,2240,165]{1,2,0:T(8,128)(2,1)} %all-gather.12.cloned.1.call-done), kind=kOutput, calls=%fused_computation.23 | convolution fusion | flops 6056878080 | bytes 27504640 | tf_op jit(solution)/shard_map/vmap()/dot_general | solution.py:126
  596.9 3.2 convert_element_type.106
  600.1 3.2 copy.29
  603.7 1.5 copy-done.9
  605.2 3.7 constant_dynamic-slice_fusion
  608.9 1.8 copy.33
  610.7 1.0 copy.32
  612.2 6.3 all-gather.8.cloned.1.call-done
  618.5 2.8 fusion.22
  621.2 28.7 %all-gather.10.cloned.1.call-done = bf16[256,5280]{1,0:T(8,128)(2,1)} async-done(((bf16[64,5280]{1,0:T(8,128)(2,1)}), bf16[256,5280]{1,0:T(8,128)(2,1)}) %all-gather.10.cloned.1.call-update) | async-done | bytes 2703376 | tf_op jit(solution)/shard_map/all_gather | solution.py:142
  649.9 2.5 multiply_reduce_fusion.2
  652.4 0.5 multiply_multiply_fusion
  652.9 0.6 copy-done.1
  653.7 0.9 copy-done.6
  654.7 1.6 fusion.23
  656.3 37.9 %reduce-scatter.4.cloned.1.call-done = bf16[64,5280]{1,0:T(8,128)(2,1)} async-done(((bf16[256,5280]{1,0:T(8,128)(2,1)}), bf16[64,5280]{1,0:T(8,128)(2,1)}) %reduce-scatter.4.cloned.1.call-update) | async-done | bytes 675856 | tf_op jit(solution)/shard_map/reduce_scatter | solution.py:128
  694.1 2.5 fusion.8
  696.6 0.9 fusion.21
  697.6 1.0 fusion.13
  698.6 0.3 copy-done.2
  698.9 0.9 copy-done.4
  699.8 0.8 multiply_reduce_fusion.1
  700.5 0.6 add_convert_fusion
  701.1 0.9 copy-done.7
  702.0 2.5 fusion.1
  704.8 4.4 fusion.24
  709.2 7.8 fusion
  717.0 29.3 %reduce-scatter.8.cloned.1.call-done = bf16[64,5280]{1,0:T(8,128)(2,1)} async-done(((bf16[256,5280]{1,0:T(8,128)(2,1)}), bf16[64,5280]{1,0:T(8,128)(2,1)}) %reduce-scatter.8.cloned.1.call-update) | async-done | bytes 675856 | tf_op jit(solution)/shard_map/reduce_scatter | solution.py:163
  746.3 4.1 reshape.80
  750.4 1.6 copy.35
  752.0 7.2 all-to-all-start.1
  759.2 31.8 %reduce-scatter.6.cloned.1.call-done = bf16[5280,64]{0,1:T(8,128)(2,1)} async-done(((bf16[5280,256]{0,1:T(8,128)(2,1)}), bf16[5280,64]{0,1:T(8,128)(2,1)}) %reduce-scatter.6.cloned.1.call-update) | async-done | bytes 675856 | tf_op jit(solution)/shard_map/reduce_scatter | solution.py:160
  791.0 4.1 reshape.79
  795.1 1.6 copy.30
  796.7 6.8 all-to-all-start
  803.5 0.8 convert_reduce_fusion
  804.3 16.9 %all-to-all-done = bf16[32,165,64]{1,2,0:T(8,128)(2,1)S(1)} async-done(((bf16[32,165,64]{1,2,0:T(8,128)(2,1)}), bf16[32,165,64]{1,2,0:T(8,128)(2,1)S(1)}, u32[]{:S(2)}, u32[]{:S(2)}) %all-to-all-start) | async-done | bytes 675872 | tf_op jit(solution)/shard_map/all_to_all | solution.py:37
  821.2 0.8 convert_reduce_fusion.1
  (48 shorter events, 1.8 us)
Async XLA Ops:
  7.2 576.9 %all-gather.12.cloned.1.call-start = ((), (), s32[]{:S(2)}) async-start(), calls=%async_computation.10 | async-start | bytes 25546752 | tf_op jit(solution)/shard_map/all_gather | solution.py:25
  7.9 610.6 %all-gather.8.cloned.1.call-start = ((), (), s32[]{:S(2)}) async-start(), calls=%async_computation.5 | async-start | bytes 3440640 | tf_op jit(solution)/shard_map/all_gather | solution.py:141
  119.7 2.9 copy-start.13
  122.6 527.4 %all-gather.10.cloned.1.call-start = ((), (), s32[]{:S(2)}) async-start(), calls=%async_computation.6 | async-start | bytes 3440640 | tf_op jit(solution)/shard_map/all_gather | solution.py:142
  225.6 4.9 copy-start.8
  230.2 463.9 %reduce-scatter.4.cloned.1.call-start = ((), (), s32[]{:S(2)}) async-start(), calls=%async_computation.7 | async-start | bytes 3440640 | tf_op jit(solution)/shard_map/reduce_scatter | solution.py:128
  230.5 2.9 copy-start.10
  603.4 1.8 copy-start.9
  603.4 142.9 %reduce-scatter.8.cloned.1.call-start = ((), (), s32[]{:S(2)}) async-start(), calls=%async_computation.9 | async-start | bytes 3440640 | tf_op jit(solution)/shard_map/reduce_scatter | solution.py:163
  608.9 1.8 copy-start.11
  608.9 2.9 copy-start.14
  608.9 2.9 copy-start.15
  611.7 38.2 %copy-start.5 = (bf16[64,5280]{1,0:T(8,128)(2,1)}, bf16[64,5280]{1,0:T(8,128)(2,1)S(1)}, u32[]{:S(2)}) copy-start(bf16[64,5280]{1,0:T(8,128)(2,1)S(1)} %copy.32) | copy-start | bytes 2027524
  652.4 1.1 copy-start.1
  652.4 2.3 copy-start.3
  653.7 0.9 copy-start.6
  654.7 39.5 %copy-start = (bf16[256,5280]{1,0:T(8,128)(2,1)S(1)}, bf16[256,5280]{1,0:T(8,128)(2,1)}, u32[]{:S(2)}) copy-start(bf16[256,5280]{1,0:T(8,128)(2,1)} %all-gather.10.cloned.1.call-done) | copy-start | bytes 8110084
  694.1 2.5 copy-start.12
  697.5 1.3 copy-start.2
  697.6 2.2 copy-start.4
  699.8 0.8 copy-start.16
  701.1 0.9 copy-start.7
  704.5 86.5 %reduce-scatter.6.cloned.1.call-start = ((), (), s32[]{:S(2)}) async-start(), calls=%async_computation.8 | async-start | bytes 3440640 | tf_op jit(solution)/shard_map/reduce_scatter | solution.py:160
  752.0 44.7 %all-to-all-start.1 = ((bf16[32,64,165]{2,1,0:T(8,128)(2,1)}), bf16[32,64,165]{2,1,0:T(8,128)(2,1)S(1)}, u32[]{:S(2)}, u32[]{:S(2)}) async-start(bf16[32,64,165]{2,1,0:T(8,128)(2,1)} %bitcast.34), calls=%async_computation.4 | async-start | bytes 2097152 | tf_op jit(solution)/shard_map/all_to_all | solution.py:37
  796.7 24.5 %all-to-all-start = ((bf16[32,165,64]{1,2,0:T(8,128)(2,1)}), bf16[32,165,64]{1,2,0:T(8,128)(2,1)S(1)}, u32[]{:S(2)}, u32[]{:S(2)}) async-start(bf16[32,165,64]{1,2,0:T(8,128)(2,1)} %copy.30), calls=%async_computation.2 | async-start | bytes 2097152 | tf_op jit(solution)/shard_map/all_to_all | solution.py:37
Sparse Core Ops, SparseCore 0:
  9.6 574.4 all-gather.11
  585.7 32.6 all-gather.7
  620.1 29.7 all-gather.9
  652.4 41.6 reduce-scatter.3
  704.6 41.6 reduce-scatter.7
  748.8 42.1 reduce-scatter.5
where the time goes:
time: 830 us; the launch traced here: 829 us
  waiting for transfers between devices  489 us (59%)
  blocking collectives  215 us (26%)
  matrix products  52.7 us (6%)
  local copies, waits for them, and re-layouts  36.8 us (4%)
  starting transfers between devices  14.9 us (2%)
  between operations  14.4 us (2%)
    all_gather x1, waiting for transfers between devices, on_gathered_pieces(): outs.append(jax.vmap(apply)(lax.all_gather(piece, axis), starts))  338 us
    all_gather x1, blocking collectives, body(): lax.all_gather(student_up, 'grp', axis=0, tiled=True)  112 us
    all_gather x1, blocking collectives, body(): lax.all_gather(student_down, 'grp', axis=1, tiled=True)  103 us
    reduce_scatter x1, waiting for transfers between devices, body(): lax.psum_scatter(on_gathered_pieces(teacher_down, 'grp', 1, columns, 1).a...  37.9 us
    reduce_scatter x1, waiting for transfers between devices, body(): lax.psum_scatter(grad_up.astype(jnp.bfloat16), 'tp', scatter_dimension=1,...  31.8 us
    reduce_scatter x1, waiting for transfers between devices, body(): lax.psum_scatter(grad_down.astype(jnp.bfloat16), 'tp', scatter_dimension=...  29.3 us
    all_gather x1, waiting for transfers between devices, body(): lax.all_gather(gathered_down, 'tp', axis=0, tiled=True)  28.7 us
    all_to_all x2, waiting for transfers between devices, sent_and_summed(): lax.all_to_all(tiles, axis, split_axis=0, concat_axis=0, tiled=True)  16.9 us
  transfers between devices with their start and end apart: 8, of which 7 were waited for; matrix products, arithmetic and copies ran while one was open for 10% of the time, Pallas kernels for 0%

commit v1 on v0

--- a/solution.py
+++ b/solution.py
@@ -135,7 +135,7 @@
     latents.append(row_state)
     gathered_up, gathered_down = (
         lax.all_gather(student_up, "grp", axis=0, tiled=True),
-        lax.all_gather(student_down, "grp", axis=1, tiled=True),
+        jnp.concatenate(lax.all_gather(student_down, "grp"), axis=1),
     )
     gathered_up, gathered_down = (
         lax.all_gather(gathered_up, "tp", axis=1, tiled=True),

time: 830 us -> 830 us (level)
  no operation moved by 1% of the time
where the time goes in v1:
time: 830 us; the launch traced here: 829 us
  waiting for transfers between devices  489 us (59%)
  blocking collectives  215 us (26%)
  matrix products  52.7 us (6%)
  local copies, waits for them, and re-layouts  36.8 us (4%)
  starting transfers between devices  14.9 us (2%)
  between operations  14.4 us (2%)
    all_gather x1, waiting for transfers between devices, on_gathered_pieces(): outs.append(jax.vmap(apply)(lax.all_gather(piece, axis), starts))  338 us
    all_gather x1, blocking collectives, body(): lax.all_gather(student_up, 'grp', axis=0, tiled=True)  112 us
    all_gather x1, blocking collectives, body(): lax.all_gather(student_down, 'grp')  103 us
    reduce_scatter x1, waiting for transfers between devices, body(): lax.psum_scatter(on_gathered_pieces(teacher_down, 'grp', 1, columns, 1).a...  37.9 us
    reduce_scatter x1, waiting for transfers between devices, body(): lax.psum_scatter(grad_up.astype(jnp.bfloat16), 'tp', scatter_dimension=1,...  31.8 us
    reduce_scatter x1, waiting for transfers between devices, body(): lax.psum_scatter(grad_down.astype(jnp.bfloat16), 'tp', scatter_dimension=...  29.3 us
    all_gather x1, waiting for transfers between devices, body(): lax.all_gather(gathered_down, 'tp', axis=0, tiled=True)  28.7 us
    all_to_all x2, waiting for transfers between devices, sent_and_summed(): lax.all_to_all(tiles, axis, split_axis=0, concat_axis=0, tiled=True)  16.9 us
  transfers between devices with their start and end apart: 8, of which 7 were waited for; matrix products, arithmetic and copies ran while one was open for 10% of the time, Pallas kernels for 0%

profile of v1, /device:TPU:0, one launch (start us, length us, event | category | flops | bytes accessed | tf_op | source)
XLA Modules:
  0.0 828.8 jit_solution(11721976496536972455)
XLA Ops:
  7.2 0.7 all-gather.12.cloned.1.call-update
  7.9 111.7 %all-gather.2 = bf16[32,165,64]{1,2,0:T(8,128)(2,1)S(1)} all-gather(bf16[1,165,64]{1,2,0:T(8,128)(2,1)} %bitcast.36), channel_id=1, replica_groups=mesh['tp'=4,'grp'=32] {'grp'}, dimensions={0}, use_global_device_ids=true | all-gather | bytes 696960 | tf_op jit(solution)/shard_map/all_gather | solution.py:137
  119.7 0.6 copy.27
  120.3 2.3 reshape.92
  122.6 103.0 %all-gather = bf16[2048,165]{1,0:T(8,128)(2,1)S(1)} all-gather(bf16[64,165]{1,0:T(8,128)(2,1)S(1)} %copy-done.13), channel_id=2, replica_groups=mesh['tp'=4,'grp'=32] {'grp'}, dimensions={0}, use_global_device_ids=true | all-gather | bytes 696960 | tf_op jit(solution)/shard_map/all_gather | solution.py:138
  225.6 1.6 copy.37
  227.1 3.1 reshape.86
  230.5 2.9 multiply_reduce_fusion
  233.4 13.2 %fusion.11 = bf16[256,2240,1]{0,1,2:T(8,128)(2,1)} fusion(bf16[5280,2240]{0,1:T(8,128)(2,1)} %param.10, bf16[256,5280]{0,1:T(8,128)(2,1)S(1)} %copy-done.8, bf16[256,5280]{0,1:T(8,128)(2,1)S(1)} %copy-done.10, f32[256]{0:T(256)S(1)} %add_rsqrt_fusion), kind=kOutput, calls=%fused_computation.22 | convolution fusion | flops 6065152000 | bytes 30209024 | tf_op jit(solution)/shard_map/dot_general | solution.py:121
  246.6 337.5 %all-gather.12.cloned.1.call-done = bf16[32,2240,165]{1,2,0:T(8,128)(2,1)} async-done(((bf16[1,2240,165]{1,2,0:T(8,128)(2,1)}), bf16[32,2240,165]{1,2,0:T(8,128)(2,1)}) %all-gather.12.cloned.1.call-update) | async-done | bytes 23654416 | tf_op jit(solution)/shard_map/all_gather | solution.py:25
  584.1 12.8 %convolution_convert_fusion = bf16[256,32,165]{0,2,1:T(8,128)(2,1)} fusion(bf16[256,2240,1]{0,1,2:T(8,128)(2,1)} %fusion.11, bf16[32,2240,165]{1,2,0:T(8,128)(2,1)} %all-gather.12.cloned.1.call-done), kind=kOutput, calls=%fused_computation.23 | convolution fusion | flops 6056878080 | bytes 27504640 | tf_op jit(solution)/shard_map/vmap()/dot_general | solution.py:126
  596.9 3.2 convert_element_type.106
  600.1 3.2 copy.29
  603.7 1.5 copy-done.9
  605.2 3.7 constant_dynamic-slice_fusion
  608.9 1.8 copy.33
  610.7 1.0 copy.32
  612.2 6.3 all-gather.8.cloned.1.call-done
  618.5 2.8 fusion.22
  621.2 28.7 %all-gather.10.cloned.1.call-done = bf16[256,5280]{1,0:T(8,128)(2,1)} async-done(((bf16[64,5280]{1,0:T(8,128)(2,1)}), bf16[256,5280]{1,0:T(8,128)(2,1)}) %all-gather.10.cloned.1.call-update) | async-done | bytes 2703376 | tf_op jit(solution)/shard_map/all_gather | solution.py:142
  649.9 2.5 multiply_reduce_fusion.2
  652.4 0.5 multiply_multiply_fusion
  652.9 0.6 copy-done.1
  653.7 0.9 copy-done.6
  654.7 1.6 fusion.23
  656.3 37.9 %reduce-scatter.4.cloned.1.call-done = bf16[64,5280]{1,0:T(8,128)(2,1)} async-done(((bf16[256,5280]{1,0:T(8,128)(2,1)}), bf16[64,5280]{1,0:T(8,128)(2,1)}) %reduce-scatter.4.cloned.1.call-update) | async-done | bytes 675856 | tf_op jit(solution)/shard_map/reduce_scatter | solution.py:128
  694.1 2.5 fusion.8
  696.6 0.9 fusion.21
  697.6 1.0 fusion.13
  698.6 0.3 copy-done.2
  698.9 0.9 copy-done.4
  699.8 0.8 multiply_reduce_fusion.1
  700.5 0.6 add_convert_fusion
  701.1 0.9 copy-done.7
  702.0 2.5 fusion.1
  704.8 4.4 fusion.24
  709.2 7.8 fusion
  717.0 29.3 %reduce-scatter.8.cloned.1.call-done = bf16[64,5280]{1,0:T(8,128)(2,1)} async-done(((bf16[256,5280]{1,0:T(8,128)(2,1)}), bf16[64,5280]{1,0:T(8,128)(2,1)}) %reduce-scatter.8.cloned.1.call-update) | async-done | bytes 675856 | tf_op jit(solution)/shard_map/reduce_scatter | solution.py:163
  746.3 4.1 reshape.88
  750.4 1.6 copy.36
  752.0 7.2 all-to-all-start.1
  759.2 31.8 %reduce-scatter.6.cloned.1.call-done = bf16[5280,64]{0,1:T(8,128)(2,1)} async-done(((bf16[5280,256]{0,1:T(8,128)(2,1)}), bf16[5280,64]{0,1:T(8,128)(2,1)}) %reduce-scatter.6.cloned.1.call-update) | async-done | bytes 675856 | tf_op jit(solution)/shard_map/reduce_scatter | solution.py:160
  791.0 4.1 reshape.87
  795.1 1.6 copy.30
  796.7 6.8 all-to-all-start
  803.5 0.8 convert_reduce_fusion
  804.3 16.9 %all-to-all-done = bf16[32,165,64]{1,2,0:T(8,128)(2,1)S(1)} async-done(((bf16[32,165,64]{1,2,0:T(8,128)(2,1)}), bf16[32,165,64]{1,2,0:T(8,128)(2,1)S(1)}, u32[]{:S(2)}, u32[]{:S(2)}) %all-to-all-start) | async-done | bytes 675872 | tf_op jit(solution)/shard_map/all_to_all | solution.py:37
  821.2 0.8 convert_reduce_fusion.1
  (48 shorter events, 1.8 us)
Async XLA Ops:
  7.2 576.9 %all-gather.12.cloned.1.call-start = ((), (), s32[]{:S(2)}) async-start(), calls=%async_computation.10 | async-start | bytes 25546752 | tf_op jit(solution)/shard_map/all_gather | solution.py:25
  7.9 610.6 %all-gather.8.cloned.1.call-start = ((), (), s32[]{:S(2)}) async-start(), calls=%async_computation.5 | async-start | bytes 3440640 | tf_op jit(solution)/shard_map/all_gather | solution.py:141
  119.7 2.9 copy-start.13
  122.6 527.4 %all-gather.10.cloned.1.call-start = ((), (), s32[]{:S(2)}) async-start(), calls=%async_computation.6 | async-start | bytes 3440640 | tf_op jit(solution)/shard_map/all_gather | solution.py:142
  225.6 4.9 copy-start.8
  230.2 463.9 %reduce-scatter.4.cloned.1.call-start = ((), (), s32[]{:S(2)}) async-start(), calls=%async_computation.7 | async-start | bytes 3440640 | tf_op jit(solution)/shard_map/reduce_scatter | solution.py:128
  230.5 2.9 copy-start.10
  603.4 1.8 copy-start.9
  603.4 142.9 %reduce-scatter.8.cloned.1.call-start = ((), (), s32[]{:S(2)}) async-start(), calls=%async_computation.9 | async-start | bytes 3440640 | tf_op jit(solution)/shard_map/reduce_scatter | solution.py:163
  608.9 1.8 copy-start.11
  608.9 2.9 copy-start.14
  608.9 2.9 copy-start.15
  611.7 38.2 %copy-start.5 = (bf16[64,5280]{1,0:T(8,128)(2,1)}, bf16[64,5280]{1,0:T(8,128)(2,1)S(1)}, u32[]{:S(2)}) copy-start(bf16[64,5280]{1,0:T(8,128)(2,1)S(1)} %copy.32) | copy-start | bytes 2027524
  652.4 1.1 copy-start.1
  652.4 2.3 copy-start.3
  653.7 0.9 copy-start.6
  654.7 39.5 %copy-start = (bf16[256,5280]{1,0:T(8,128)(2,1)S(1)}, bf16[256,5280]{1,0:T(8,128)(2,1)}, u32[]{:S(2)}) copy-start(bf16[256,5280]{1,0:T(8,128)(2,1)} %all-gather.10.cloned.1.call-done) | copy-start | bytes 8110084
  694.1 2.5 copy-start.12
  697.5 1.3 copy-start.2
  697.6 2.2 copy-start.4
  699.8 0.8 copy-start.16
  701.1 0.9 copy-start.7
  704.5 86.5 %reduce-scatter.6.cloned.1.call-start = ((), (), s32[]{:S(2)}) async-start(), calls=%async_computation.8 | async-start | bytes 3440640 | tf_op jit(solution)/shard_map/reduce_scatter | solution.py:160
  752.0 44.7 %all-to-all-start.1 = ((bf16[32,64,165]{2,1,0:T(8,128)(2,1)}), bf16[32,64,165]{2,1,0:T(8,128)(2,1)S(1)}, u32[]{:S(2)}, u32[]{:S(2)}) async-start(bf16[32,64,165]{2,1,0:T(8,128)(2,1)} %bitcast.31), calls=%async_computation.4 | async-start | bytes 2097152 | tf_op jit(solution)/shard_map/all_to_all | solution.py:37
  796.7 24.5 %all-to-all-start = ((bf16[32,165,64]{1,2,0:T(8,128)(2,1)}), bf16[32,165,64]{1,2,0:T(8,128)(2,1)S(1)}, u32[]{:S(2)}, u32[]{:S(2)}) async-start(bf16[32,165,64]{1,2,0:T(8,128)(2,1)} %copy.30), calls=%async_computation.2 | async-start | bytes 2097152 | tf_op jit(solution)/shard_map/all_to_all | solution.py:37
Sparse Core Ops, SparseCore 0:
  9.6 574.4 all-gather.11
  585.7 32.6 all-gather.7
  620.1 29.7 all-gather.9
  652.4 41.6 reduce-scatter.3
  704.6 41.6 reduce-scatter.7
  748.8 42.1 reduce-scatter.5
